TPU v7x, 512 devices: a whole 4x8x8 slice. The times are simulated.
512 devices in a mesh: row: 32 (over y_hi, x, core), col: 16 (over y_lo, z).
Axes of the slice: x: 4, y: 8 (y_hi: 4, y_lo: 2; y = y_hi * 2 + y_lo), z: 8, core: 2. Of those that a mesh axis runs over, the one named last changes fastest.
Arguments:
- amplitudes: bfloat16 [1024, 32768], P('row', 'col'), may hold values from -6 to 6
- integrals: bfloat16 [32768, 32768], P('col', 'row'), may hold values from -0.0390625 to 0.0390625
- tile_mask: int32 [256, 256], P('col', 'row'), may hold values 0 or 1
- driving: bfloat16 [1024, 32768], P('col', 'row'), may hold values from -6 to 6
- occupied_energy: float32 [1024], P('col'), may hold values from -1.5 to -0.5
- virtual_energy: float32 [32768], P('row'), may hold values from 0.5 to 2.5
Outputs:
- update: float32 [1024, 32768], P('col', 'row')
All inputs are finite; a program needn't handle non-finite values. No bound on the sum of `tile_mask` on one device may be relied on, other than what follows from the above.
Results may differ from a plain program's by a relative error of at most 0.0003.
Values may be sent and summed in bfloat16 or wider, within the bound.
A program may use at most 64 MiB of HBM per device.

v0:
```python
import jax
import jax.numpy as jnp
from jax import lax
from jax.sharding import PartitionSpec as P


def shards(amplitudes, integrals, tile_mask, driving, occupied_energy, virtual_energy):
    tiles_in = tile_mask.shape[0]
    tiles_out = tile_mask.shape[1]
    tile_size = integrals.shape[0] // tiles_in
    shaped = integrals.reshape(tiles_in, tile_size, tiles_out, tile_size)
    masked = (shaped * tile_mask.astype(jnp.bfloat16)[:, None, :, None]).reshape(integrals.shape)
    partial_sum = jnp.dot(
        lax.all_gather(amplitudes, "row", axis=0, tiled=True),
        masked,
        preferred_element_type=jnp.float32,
    )
    ladder = lax.psum_scatter(partial_sum, "col", scatter_dimension=0, tiled=True)
    denom = virtual_energy[None, :] - occupied_energy[:, None]
    return (driving.astype(jnp.float32) + ladder) / denom


def solution(mesh):
    in_specs = (
        P("row", "col"),
        P("col", "row"),
        P("col", "row"),
        P("col", "row"),
        P("col"),
        P("row"),
    )
    out_specs = P("col", "row")
    return jax.shard_map(shards, mesh=mesh, in_specs=in_specs, out_specs=out_specs, check_vma=False)
```

profile of v0, /device:TPU:2, one launch (start us, length us, event | category | flops | bytes accessed | tf_op | source)
XLA Modules:
  0.0 188.9 jit_solution(5905273928543527825)
XLA Ops:
  6.5 0.0 all-gather.2.cloned.1.call-start
  6.5 0.7 all-gather.2.cloned.1.call-update
  7.3 0.0 reduce-scatter.4.cloned.1.call-start
  7.3 0.7 convert_element_type.7
  8.0 0.1 copy.13
  8.1 72.6 %all-gather.2.cloned.1.call-done = bf16[1024,2048]{1,0:T(8,128)(2,1)} async-done(((bf16[32,2048]{1,0:T(8,128)(2,1)}), bf16[1024,2048]{1,0:T(8,128)(2,1)}) %all-gather.2.cloned.1.call-update) | async-done | bytes 4194320 | tf_op jit(solution)/shard_map/all_gather | solution.py:14
  80.7 0.0 copy-start.3
  80.7 0.6 mul.11
  81.3 1.6 copy-done.3
  82.9 8.8 %fusion.2 = f32[1024,1024]{0,1:T(8,128)} fusion(bf16[1024,2048]{1,0:T(8,128)(2,1)} %all-gather.2.cloned.1.call-done, bf16[2048,1024]{1,0:T(8,128)(2,1)S(1)} %copy-done.3, bf16[256,8,8,128]{3,2,1,0:T(8,128)(2,1)S(1)} %bitcast.11), kind=kOutput, calls=%fused_computation.3 | convolution fusion | flops 4297064448 | bytes 16777216 | tf_op jit(solution)/shard_map/dot_general | solution.py:13
  91.7 5.4 %copy.15 = f32[1024,1024]{1,0:T(8,128)} copy(f32[1024,1024]{0,1:T(8,128)} %fusion.2) | data formatting | bytes 8388608
  97.1 0.0 copy-start
  97.1 0.0 copy-start.1
  97.1 0.0 copy-start.2
  97.1 0.0 reduce-scatter.4.cloned.1.call-update
  97.1 83.2 %reduce-scatter.4.cloned.1.call-done = f32[64,1024]{1,0:T(8,128)} async-done(((f32[1024,1024]{1,0:T(8,128)}), f32[64,1024]{1,0:T(8,128)}) %reduce-scatter.4.cloned.1.call-update) | async-done | bytes 262160 | tf_op jit(solution)/shard_map/reduce_scatter | solution.py:18
  180.3 0.0 copy-done
  180.3 0.0 copy-done.1
  180.3 0.0 copy-done.2
  180.3 1.8 subtract_divide_fusion
Async XLA Ops:
  6.5 74.2 %all-gather.2.cloned.1.call-start = ((), (), s32[]{:S(2)}) async-start(), calls=%async_computation.1 | async-start | bytes 4325376 | tf_op jit(solution)/shard_map/all_gather | solution.py:14
  7.3 173.1 %reduce-scatter.4.cloned.1.call-start = ((), (), s32[]{:S(2)}) async-start(), calls=%async_computation.2 | async-start | bytes 4456448 | tf_op jit(solution)/shard_map/reduce_scatter | solution.py:18
  80.7 2.2 %copy-start.3 = (bf16[2048,1024]{1,0:T(8,128)(2,1)S(1)}, bf16[2048,1024]{1,0:T(8,128)(2,1)}, u32[]{:S(2)}) copy-start(bf16[2048,1024]{1,0:T(8,128)(2,1)} %param.7) | copy-start | bytes 12582916
  97.1 83.3 %copy-start = (bf16[64,1024]{1,0:T(8,128)(2,1)S(1)}, bf16[64,1024]{1,0:T(8,128)(2,1)}, u32[]{:S(2)}) copy-start(bf16[64,1024]{1,0:T(8,128)(2,1)} %param.9) | copy-start | bytes 393220
  97.1 83.3 %copy-start.1 = (f32[1024]{0:T(1024)S(1)}, f32[1024]{0:T(1024)}, u32[]{:S(2)}) copy-start(f32[1024]{0:T(1024)} %param.11) | copy-start | bytes 12292
  97.1 83.3 %copy-start.2 = (f32[64]{0:T(128)S(1)}, f32[64]{0:T(128)}, u32[]{:S(2)}) copy-start(f32[64]{0:T(128)} %param.10) | copy-start | bytes 772
Sparse Core Ops, SparseCore 0:
  10.5 70.1 all-gather.1
  97.2 83.0 reduce-scatter.3
where the time goes:
time: 189 us
  waiting for transfers between devices  157 us (83%)
  between operations  13.4 us (7%)
  matrix products  8.82 us (5%)
  local copies, waits for them, and re-layouts  7.65 us (4%)
  other arithmetic  2.45 us (1%)
    reduce_scatter x1, waiting for transfers between devices, shards(): lax.psum_scatter(partial_sum, 'col', scatter_dimension=0, tiled=True)  83.2 us
    all_gather x1, waiting for transfers between devices, shards(): lax.all_gather(amplitudes, 'row', axis=0, tiled=True)  72.6 us
    dot_general x1, matrix products, shards(): jnp.dot(lax.all_gather(amplitudes, 'row', axis=0, tiled=True), masked, pr...  8.82 us
    unnamed x9, local copies, waits for them, and re-layouts  6.95 us
  transfers between devices with their start and end apart: 2, of which 2 were waited for; matrix products, arithmetic and copies ran while one was open for 0% of the time, Pallas kernels for 0%

commit v1 on v0

--- a/solution.py
+++ b/solution.py
@@ -11,7 +11,9 @@
     shaped = integrals.reshape(tiles_in, tile_size, tiles_out, tile_size)
     masked = (shaped * tile_mask.astype(jnp.bfloat16)[:, None, :, None]).reshape(integrals.shape)
     partial_sum = jnp.dot(
-        lax.all_gather(amplitudes, "row", axis=0, tiled=True),
+        jnp.concatenate(
+            lax.all_to_all(jnp.stack([amplitudes] * lax.axis_size("row")), "row", 0, 0), axis=0
+        ),
         masked,
         preferred_element_type=jnp.float32,
     )

time: 189 us -> 228 us (1.21)
  the two profiles are of different devices: /device:TPU:2 before, /device:TPU:6 now
where the time goes in v1:
time: 228 us
  waiting for transfers between devices  182 us (80%)
  between operations  13.4 us (6%)
  local copies, waits for them, and re-layouts  11 us (5%)
  starting transfers between devices  10.5 us (5%)
  matrix products  8.89 us (4%)
    all_to_all x1, waiting for transfers between devices, shards(): lax.all_to_all(jnp.stack([amplitudes] * lax.axis_size('row')), 'row', 0, 0)  96.7 us
    reduce_scatter x1, waiting for transfers between devices, shards(): lax.psum_scatter(partial_sum, 'col', scatter_dimension=0, tiled=True)  85.8 us
    all_to_all x1, starting transfers between devices, shards(): lax.all_to_all(jnp.stack([amplitudes] * lax.axis_size('row')), 'row', 0, 0)  10.4 us
    dot_general x1, matrix products, shards(): jnp.dot(jnp.concatenate(lax.all_to_all(jnp.stack([amplitudes] * lax.axis_...  8.89 us
    unnamed x11, local copies, waits for them, and re-layouts  6.94 us
  transfers between devices with their start and end apart: 2, of which 2 were waited for; matrix products, arithmetic and copies ran while one was open for 0% of the time, Pallas kernels for 0%

profile of v1, /device:TPU:6, one launch (start us, length us, event | category | flops | bytes accessed | tf_op | source)
XLA Modules:
  0.0 228.1 jit_solution(650126198629270228)
XLA Ops:
  6.5 3.4 %stack.2 = bf16[32,32,2048]{2,1,0:T(8,128)(2,1)} broadcast(bf16[32,2048]{1,0:T(8,128)(2,1)} %param.6), dimensions={1,2} | broadcast | bytes 4325376 | tf_op jit(solution)/shard_map/stack | solution.py:15
  9.9 0.0 copy-start.2
  9.9 10.4 %all-to-all-start = ((bf16[32,32,2048]{2,1,0:T(8,128)(2,1)}), bf16[32,32,2048]{2,1,0:T(8,128)(2,1)}, u32[]{:S(2)}, u32[]{:S(2)}) async-start(bf16[32,32,2048]{2,1,0:T(8,128)(2,1)} %stack.2), calls=%async_computation | async-start | bytes 8388608 | tf_op jit(solution)/shard_map/all_to_all | solution.py:15
  20.4 0.0 reduce-scatter.4.cloned.1.call-start
  20.4 0.0 copy-done.2
  20.5 0.1 copy.13
  20.5 96.7 %all-to-all-done = bf16[32,32,2048]{2,1,0:T(8,128)(2,1)} async-done(((bf16[32,32,2048]{2,1,0:T(8,128)(2,1)}), bf16[32,32,2048]{2,1,0:T(8,128)(2,1)}, u32[]{:S(2)}, u32[]{:S(2)}) %all-to-all-start) | async-done | bytes 4194336 | tf_op jit(solution)/shard_map/all_to_all | solution.py:15
  117.2 0.0 copy-start.4
  117.2 0.6 mul.11
  117.8 1.6 copy-done.4
  119.4 8.9 %fusion.2 = f32[1024,1024]{0,1:T(8,128)} fusion(bf16[1024,2048]{1,0:T(8,128)(2,1)} %bitcast, bf16[2048,1024]{1,0:T(8,128)(2,1)S(1)} %copy-done.4, bf16[256,8,8,128]{3,2,1,0:T(8,128)(2,1)S(1)} %bitcast.12), kind=kOutput, calls=%fused_computation.3 | convolution fusion | flops 4297064448 | bytes 16777216 | tf_op jit(solution)/shard_map/dot_general | solution.py:13
  128.3 5.4 %copy.15 = f32[1024,1024]{1,0:T(8,128)} copy(f32[1024,1024]{0,1:T(8,128)} %fusion.2) | data formatting | bytes 8388608
  133.6 0.0 copy-start
  133.6 0.0 copy-start.1
  133.6 0.0 copy-start.3
  133.6 0.0 reduce-scatter.4.cloned.1.call-update
  133.7 85.8 %reduce-scatter.4.cloned.1.call-done = f32[64,1024]{1,0:T(8,128)} async-done(((f32[1024,1024]{1,0:T(8,128)}), f32[64,1024]{1,0:T(8,128)}) %reduce-scatter.4.cloned.1.call-update) | async-done | bytes 262160 | tf_op jit(solution)/shard_map/reduce_scatter | solution.py:20
  219.4 0.0 copy-done
  219.5 0.0 copy-done.1
  219.5 0.0 copy-done.3
  219.5 1.8 subtract_divide_fusion
  (1 shorter events, 0.0 us)
Async XLA Ops:
  9.9 10.5 %copy-start.2 = (s32[16,8]{0,1:T(8,128)S(1)}, s32[16,8]{0,1:T(8,128)}, u32[]{:S(2)}) copy-start(s32[16,8]{0,1:T(8,128)} %param.8) | copy-start | bytes 1540
  9.9 107.3 %all-to-all-start = ((bf16[32,32,2048]{2,1,0:T(8,128)(2,1)}), bf16[32,32,2048]{2,1,0:T(8,128)(2,1)}, u32[]{:S(2)}, u32[]{:S(2)}) async-start(bf16[32,32,2048]{2,1,0:T(8,128)(2,1)} %stack.2), calls=%async_computation | async-start | bytes 8388608 | tf_op jit(solution)/shard_map/all_to_all | solution.py:15
  20.4 199.1 %reduce-scatter.4.cloned.1.call-start = ((), (), s32[]{:S(2)}) async-start(), calls=%async_computation.2 | async-start | bytes 4456448 | tf_op jit(solution)/shard_map/reduce_scatter | solution.py:20
  117.2 2.2 copy-start.4
  133.6 85.8 %copy-start = (bf16[64,1024]{1,0:T(8,128)(2,1)S(1)}, bf16[64,1024]{1,0:T(8,128)(2,1)}, u32[]{:S(2)}) copy-start(bf16[64,1024]{1,0:T(8,128)(2,1)} %param.9) | copy-start | bytes 393220
  133.6 85.8 %copy-start.1 = (f32[1024]{0:T(1024)S(1)}, f32[1024]{0:T(1024)}, u32[]{:S(2)}) copy-start(f32[1024]{0:T(1024)} %param.11) | copy-start | bytes 12292
  133.6 85.8 %copy-start.3 = (f32[64]{0:T(128)S(1)}, f32[64]{0:T(128)}, u32[]{:S(2)}) copy-start(f32[64]{0:T(128)} %param.10) | copy-start | bytes 772
Sparse Core Ops, SparseCore 0:
  133.8 85.6 reduce-scatter.3
